TPU v7x, 32 devices: a 4x4x1 block of a 4x4x8 slice. The times are simulated.
32 devices in a mesh: dp: 1 (over z), ing: 4 (over y), grp: 8 (over x, core).
Axes of the slice: x: 4, y: 4, z: 1, core: 2. Of those that a mesh axis runs over, the one named last changes fastest.
The devices are a block of a 4x4x8 slice.
Arguments:
- tokens: bfloat16 [4096, 2560], P(('dp', 'grp', 'ing'))
- expert_ids: int32 [4096, 3, 2], P(('dp', 'grp', 'ing'))
- gate_vals: float32 [4096, 3, 2], P(('dp', 'grp', 'ing'))
- w_one: bfloat16 [64, 2560, 1536], P(('grp', 'ing'))
- w_three: bfloat16 [64, 2560, 1536], P(('grp', 'ing'))
- w_two: bfloat16 [64, 1536, 2560], P(('grp', 'ing'))
Outputs:
- output: bfloat16 [4096, 2560], P(('dp', 'grp', 'ing'))
All inputs are finite; a program needn't handle non-finite values.
Results may differ from a plain program's by a relative error of at most 0.00128.
Values are sent between devices in bfloat16 or wider.
A program may use at most 768 MiB of HBM per device.

v0:
```python
import jax
import jax.numpy as jnp
from jax import lax
from jax.sharding import PartitionSpec as P


def solution(mesh):
    grp_size = mesh.shape['grp']
    ing_size = mesh.shape['ing']
    row_spec = P(('dp', 'grp', 'ing'))
    exp_spec = P(('grp', 'ing'))

    def local_fn(tokens, expert_ids, gate_vals, w_one, w_three, w_two):
        tok_count, d_model = tokens.shape
        m_groups = expert_ids.shape[1]
        per_group = expert_ids.shape[2]
        top_k = m_groups * per_group
        exp_local = w_one.shape[0]
        exp_group = exp_local * ing_size
        n_experts = exp_group * grp_size
        cap_group = (tok_count * m_groups + grp_size - 1) // grp_size
        cap_exp = (cap_group * per_group + exp_group - 1) // exp_group

        tok_grp = expert_ids[:, :, 0] // exp_group
        grp_sel = jnp.any(tok_grp[:, :, None] == jnp.arange(grp_size), axis=1)
        sel_int = grp_sel.astype(jnp.int32)
        grp_slot = jnp.cumsum(sel_int, axis=0) - sel_int
        src_mask = grp_sel[:, :, None] & (grp_slot[:, :, None] == jnp.arange(cap_group))
        src_hot = src_mask.astype(jnp.bfloat16)
        flat_ids = expert_ids.reshape(tok_count, top_k)
        flat_gate = gate_vals.reshape(tok_count, top_k)
        gate_dense = jnp.sum(jnp.where(flat_ids[:, :, None] == jnp.arange(n_experts), flat_gate[:, :, None], 0.0), axis=1)
        gate_dense = gate_dense.reshape(tok_count, grp_size, exp_group)
        x_send = jnp.einsum('trc,td->rcd', src_hot, tokens, preferred_element_type=jnp.float32).astype(jnp.bfloat16)
        g_send = jnp.einsum('trc,tre->rce', src_mask.astype(jnp.float32), gate_dense, precision=lax.Precision.HIGHEST, preferred_element_type=jnp.float32)
        x_recv = lax.all_to_all(x_send, 'grp', 0, 0, tiled=True)
        g_recv = lax.all_to_all(g_send, 'grp', 0, 0, tiled=True)

        chosen = g_recv != 0.0
        chosen_int = chosen.astype(jnp.int32)
        exp_slot = jnp.cumsum(chosen_int, axis=1) - chosen_int
        fwd_mask = chosen[..., None] & (exp_slot[..., None] == jnp.arange(cap_exp))
        fwd_mask = fwd_mask.reshape(grp_size, cap_group, ing_size, exp_local, cap_exp)
        x_fan = jnp.einsum('scjlq,scd->ljsqd', fwd_mask.astype(jnp.bfloat16), x_recv, preferred_element_type=jnp.float32).astype(jnp.bfloat16)
        x_exp = lax.all_to_all(x_fan, 'ing', 1, 1, tiled=True)

        exp_rows = x_exp.reshape(exp_local, ing_size * grp_size * cap_exp, d_model)
        h_one = jnp.einsum('lrd,ldf->lrf', exp_rows, w_one, preferred_element_type=jnp.float32)
        h_three = jnp.einsum('lrd,ldf->lrf', exp_rows, w_three, preferred_element_type=jnp.float32)
        act_bf = (jax.nn.silu(h_one) * h_three).astype(jnp.bfloat16)
        exp_out = jnp.einsum('lrf,lfd->lrd', act_bf, w_two, preferred_element_type=jnp.float32).astype(jnp.bfloat16)
        exp_out = exp_out.reshape(exp_local, ing_size, grp_size, cap_exp, d_model)

        x_back = lax.all_to_all(exp_out, 'ing', 1, 1, tiled=True)
        weights = fwd_mask.astype(jnp.float32) * g_recv.reshape(grp_size, cap_group, ing_size, exp_local)[..., None]
        grp_sum = jnp.einsum('scjlq,ljsqd->scd', weights, x_back, precision=lax.Precision.HIGHEST, preferred_element_type=jnp.float32).astype(jnp.bfloat16)
        y_back = lax.all_to_all(grp_sum, 'grp', 0, 0, tiled=True)
        return jnp.einsum('trc,rcd->td', src_hot, y_back, preferred_element_type=jnp.float32).astype(jnp.bfloat16)

    return jax.shard_map(local_fn, mesh=mesh, in_specs=(row_spec, row_spec, row_spec, exp_spec, exp_spec, exp_spec), out_specs=row_spec, check_vma=False)
```

profile of v0, /device:TPU:97, one launch (start us, length us, event | category | flops | bytes accessed | tf_op | source)
XLA Modules:
  0.0 225.7 jit_solution(2542492804717767411)
XLA Ops:
  0.0 0.0 copy-start
  0.0 0.8 and_select_fusion
  0.8 0.7 eq.66
  1.5 0.7 broadcast_in_dim.14
  2.2 0.1 copy.63
  2.3 0.2 reduce_window_sum.22
  2.6 0.2 fusion.36
  2.8 0.7 reshape.39
  3.5 6.0 %all-to-all-start = ((f32[8,1,384]{2,1,0:T(1,128)}), f32[8,1,384]{2,1,0:T(1,128)S(1)}, u32[]{:S(2)}, u32[]{:S(2)}) async-start(f32[8,1,384]{2,1,0:T(1,128)} %reshape.39), calls=%async_computation | async-start | bytes 24576 | tf_op jit(solution)/shard_map/all_to_all | solution.py:37
  9.5 0.0 copy-done
  9.6 1.9 convolution_convert_fusion.2
  11.5 2.5 %all-to-all-done = f32[8,1,384]{2,1,0:T(1,128)S(1)} async-done(((f32[8,1,384]{2,1,0:T(1,128)}), f32[8,1,384]{2,1,0:T(1,128)S(1)}, u32[]{:S(2)}, u32[]{:S(2)}) %all-to-all-start) | async-done | bytes 12320 | tf_op jit(solution)/shard_map/all_to_all | solution.py:37
  14.0 4.2 %all-to-all-start.1 = ((bf16[8,48,2560]{2,1,0:T(8,128)(2,1)}), bf16[8,48,2560]{2,1,0:T(8,128)(2,1)S(1)}, u32[]{:S(2)}, u32[]{:S(2)}) async-start(bf16[8,48,2560]{2,1,0:T(8,128)(2,1)} %convolution_convert_fusion.2), calls=%async_computation.1 | async-start | bytes 3932160 | tf_op jit(solution)/shard_map/all_to_all | solution.py:36
  18.2 0.5 broadcast.30
  18.7 0.7 reduce
  19.4 0.1 reshape.40
  19.5 0.1 copy.68
  19.7 3.8 %fusion.41 = s32[8,48,8]{2,0,1:T(8,128)S(1)} fusion(s32[8,48,8]{2,0,1:T(8,128)S(1)} %copy.68), kind=kOutput, calls=%fused_computation.46 | output fusion | flops 144384 | bytes 24576 | tf_op jit(solution)/shard_map/jit(cumsum)/reduce_window_sum | solution.py:41
  23.4 0.1 copy.69
  23.5 19.3 %all-to-all-done.1 = bf16[8,48,2560]{2,1,0:T(8,128)(2,1)S(1)} async-done(((bf16[8,48,2560]{2,1,0:T(8,128)(2,1)}), bf16[8,48,2560]{2,1,0:T(8,128)(2,1)S(1)}, u32[]{:S(2)}, u32[]{:S(2)}) %all-to-all-start.1) | async-done | bytes 1966112 | tf_op jit(solution)/shard_map/all_to_all | solution.py:36
  42.9 1.5 fusion.2
  44.4 2.2 copy.73
  46.6 49.8 %all_to_all.25 = bf16[2,4,8,12,2560]{4,2,3,0,1:T(8,128)(2,1)S(1)} all-to-all(bf16[2,4,8,12,2560]{4,2,3,0,1:T(8,128)(2,1)S(1)} %copy.73), channel_id=1, replica_groups=mesh['dp'=1,'ing'=4,'grp'=8] {'ing'}, dimensions={1} | all-to-all | bytes 7864320 | tf_op jit(solution)/shard_map/all_to_all | solution.py:45
  96.5 4.0 %copy.74 = bf16[2,4,8,12,2560]{4,0,3,2,1:T(2,128)(2,1)S(1)} copy(bf16[2,4,8,12,2560]{4,2,3,0,1:T(8,128)(2,1)S(1)} %all_to_all.25) | data formatting | bytes 7864320 | tf_op jit(solution)/shard_map/all_to_all | solution.py:45
  100.5 0.0 copy-start.2
  100.5 1.9 copy-done.2
  102.4 11.8 %fusion.11 = f32[2,384,1536]{2,1,0:T(8,128)} fusion(bf16[2,2560,1536]{2,1,0:T(8,128)(2,1)} %param.9, bf16[2,384,2560]{2,0,1:T(2,128)(2,1)S(1)} %bitcast.52), kind=kOutput, calls=%fused_computation.12 | convolution fusion | flops 6039797760 | bytes 24379392 | tf_op jit(solution)/shard_map/lrd,ldf->lrf/dot_general | solution.py:48
  114.2 21.3 %convolution_convert_fusion.1 = bf16[2,384,2560]{2,1,0:T(8,128)(2,1)} fusion(bf16[2,1536,2560]{2,1,0:T(8,128)(2,1)} %param.11, f32[2,384,1536]{2,1,0:T(8,128)} %fusion.11, bf16[2,2560,1536]{2,1,0:T(8,128)(2,1)} %param.10, bf16[2,384,2560]{2,0,1:T(2,128)(2,1)} %bitcast.53), kind=kOutput, calls=%fused_computation.3 | convolution fusion | flops 12088639488 | bytes 44040192 | tf_op jit(solution)/shard_map/lrf,lfd->lrd/dot_general | solution.py:51
  135.5 6.2 %copy.77 = bf16[2,384,2560]{2,0,1:T(2,128)(2,1)S(1)} copy(bf16[2,384,2560]{2,1,0:T(8,128)(2,1)} %convolution_convert_fusion.1) | data formatting | bytes 7864320 | tf_op jit(solution)/shard_map/convert_element_type | solution.py:51
  141.6 1.2 copy.78
  142.8 46.1 %all_to_all.26 = bf16[2,4,8,12,2560]{4,2,3,0,1:T(8,128)(2,1)S(1)} all-to-all(bf16[2,4,8,12,2560]{4,2,3,0,1:T(8,128)(2,1)S(1)} %copy.78), channel_id=1, replica_groups=mesh['dp'=1,'ing'=4,'grp'=8] {'ing'}, dimensions={1} | all-to-all | bytes 7864320 | tf_op jit(solution)/shard_map/all_to_all | solution.py:54
  188.9 0.0 copy-start.1
  188.9 4.5 %fusion.6 = bf16[8,48,2560]{2,1,0:T(8,128)(2,1)S(1)} fusion(bf16[2,4,8,12,2560]{4,2,3,0,1:T(8,128)(2,1)S(1)} %all_to_all.26, pred[8,48,4,2]{1,3,0,2:T(4,128)(4,1)S(1)} %copy.67, f32[8,48,4,2]{1,3,2,0:T(2,128)S(1)} %bitcast.54, s32[8,48,4,2]{1,3,2,0:T(2,128)S(1)} %bitcast.56), kind=kOutput, calls=%fused_computation.8 | convolution fusion | flops 1133555712 | bytes 5925888 | tf_op jit(solution)/shard_map/scjlq,ljsqd->scd/dot_general | solution.py:56
  193.4 30.9 %all_to_all.27 = bf16[8,48,2560]{2,1,0:T(8,128)(2,1)S(1)} all-to-all(bf16[8,48,2560]{2,1,0:T(8,128)(2,1)S(1)} %fusion.6), channel_id=1, replica_groups=mesh['dp'=1,'ing'=4,'grp'=8] {'grp'}, dimensions={0} | all-to-all | bytes 3932160 | tf_op jit(solution)/shard_map/all_to_all | solution.py:57
  224.3 1.4 fusion.9
  225.7 0.0 copy-done.1
  (10 shorter events, 0.2 us)
Async XLA Ops:
  0.0 9.6 %copy-start = (bf16[128,2560]{1,0:T(8,128)(2,1)S(1)}, bf16[128,2560]{1,0:T(8,128)(2,1)}, u32[]{:S(2)}) copy-start(bf16[128,2560]{1,0:T(8,128)(2,1)} %param.6) | copy-start | bytes 1966084
  3.5 10.4 %all-to-all-start = ((f32[8,1,384]{2,1,0:T(1,128)}), f32[8,1,384]{2,1,0:T(1,128)S(1)}, u32[]{:S(2)}, u32[]{:S(2)}) async-start(f32[8,1,384]{2,1,0:T(1,128)} %reshape.39), calls=%async_computation | async-start | bytes 24576 | tf_op jit(solution)/shard_map/all_to_all | solution.py:37
  14.0 28.9 %all-to-all-start.1 = ((bf16[8,48,2560]{2,1,0:T(8,128)(2,1)}), bf16[8,48,2560]{2,1,0:T(8,128)(2,1)S(1)}, u32[]{:S(2)}, u32[]{:S(2)}) async-start(bf16[8,48,2560]{2,1,0:T(8,128)(2,1)} %convolution_convert_fusion.2), calls=%async_computation.1 | async-start | bytes 3932160 | tf_op jit(solution)/shard_map/all_to_all | solution.py:36
  100.5 1.9 copy-start.2
  188.9 36.8 %copy-start.1 = (bf16[128,2560]{1,0:T(8,128)(2,1)S(1)}, bf16[128,2560]{1,0:T(8,128)(2,1)}, u32[]{:S(2)}) copy-start(bf16[128,2560]{1,0:T(8,128)(2,1)} %param.6) | copy-start | bytes 1966084
where the time goes:
time: 226 us
  blocking collectives  127 us (56%)
  matrix products  42.6 us (19%)
  waiting for transfers between devices  21.8 us (10%)
  local copies, waits for them, and re-layouts  18.6 us (8%)
  starting transfers between devices  10.2 us (5%)
  other arithmetic  5.46 us (2%)
    all_to_all x1, blocking collectives, local_fn(): x_exp = lax.all_to_all(x_fan, 'ing', 1, 1, tiled=True)  49.8 us
    all_to_all x1, blocking collectives, local_fn(): x_back = lax.all_to_all(exp_out, 'ing', 1, 1, tiled=True)  46.1 us
    all_to_all x1, blocking collectives, local_fn(): y_back = lax.all_to_all(grp_sum, 'grp', 0, 0, tiled=True)  30.9 us
    dot_general x1, matrix products, local_fn(): jnp.einsum('lrf,lfd->lrd', act_bf, w_two, preferred_element_type=jnp.floa...  21.3 us
    all_to_all x1, waiting for transfers between devices, local_fn(): x_recv = lax.all_to_all(x_send, 'grp', 0, 0, tiled=True)  19.3 us
    dot_general x1, matrix products, local_fn(): jnp.einsum('lrd,ldf->lrf', exp_rows, w_one, preferred_element_type=jnp.fl...  11.8 us
    convert_element_type x1, local copies, waits for them, and re-layouts, local_fn(): jnp.einsum('lrf,lfd->lrd', act_bf, w_two, preferred_element_type=jnp.floa...  6.16 us
    all_to_all x1, starting transfers between devices, local_fn(): g_recv = lax.all_to_all(g_send, 'grp', 0, 0, tiled=True)  6.01 us
  transfers between devices with their start and end apart: 2, of which 2 were waited for; matrix products, arithmetic and copies ran while one was open for 3% of the time, Pallas kernels for 0%

commit v1 on v0

v1 whole, which is shorter than its diff:
```python
import functools

import jax
import jax.numpy as jnp
from jax import lax
from jax.experimental import pallas as pl
from jax.experimental.pallas import tpu as pltpu
from jax.sharding import PartitionSpec as P

BF = jnp.bfloat16
F32 = jnp.float32
MESH = pl.DeviceIdType.MESH
NC = 2
NT = (((1,), (1,)), ((), ()))


def dot(a, b):
    return jnp.dot(a, b, preferred_element_type=F32)


def dot_nt(a, b):
    return lax.dot_general(a, b, NT, preferred_element_type=F32)


def wait_bytes(ref, sem):
    pltpu.make_async_copy(ref, ref, sem).wait()


def moe_kernel(dims, tok_hbm, meta_ref, perm_ref, w1_hbm, w3_hbm, w2_hbm, y_ref,
               wa, wb, ag, ymeta, xmeta, sel, xin, act, actp, out, eb, gsum, grec,
               smat, cmat, fmat,
               wa_sem, wb_sem, tok_sem, meta_send, ymeta_recv, xmeta_recv,
               own_send, fwd_send, dn_recv, up_recv, far_recv,
               disp_send, disp_recv, comb_send, comb_recv, fin_send, fin_recv):
    (t_cnt, d_model, ff, nx, ny, e_loc, e_grp, cap_g, cap_e, top_k, cw) = dims
    nk = d_model // cw
    nd = nx * NC
    rows = nd * ny * cap_e
    grp = lax.axis_index('grp')
    j = lax.axis_index('ing')
    x = grp // NC
    c = grp % NC

    def at(dx, dc, dj):
        gx = lax.rem(x + dx, nx)
        cc = c if dc == 0 else (NC - 1) - c
        return gx * NC + cc, lax.rem(j + dj, ny)

    def dev(dx, dc, dj):
        gg, jj = at(dx, dc, dj)
        return {'grp': gg, 'ing': jj}

    def send(src, dst, ssem, rsem, where):
        pltpu.make_async_remote_copy(src_ref=src, dst_ref=dst, send_sem=ssem, recv_sem=rsem,
                                     device_id=dev(*where), device_id_type=MESH).start()

    def cols(k):
        return pl.ds(k * cw, cw)

    row_peers = [(dx, dc, 0) for dx in range(nx) for dc in range(NC) if dx or dc]
    col_peers = [(0, dc, dj) for dj in range(ny) for dc in range(NC) if dj or dc]
    far_first = sorted(row_peers, key=lambda p: -min(p[0], nx - p[0]))
    col_far_first = sorted(col_peers, key=lambda p: -min(p[2], ny - p[2]))

    tok_cp = pltpu.make_async_copy(tok_hbm, ag.at[0], tok_sem)
    tok_cp.start()
    wcopies = {}

    def load_w(name, src, dst, sem):
        cp = pltpu.make_async_copy(src, dst, sem)
        cp.start()
        wcopies[name] = cp

    load_w('1_0', w1_hbm.at[0], wa.at[0], wa_sem.at[0])
    load_w('3_0', w3_hbm.at[0], wa.at[1], wa_sem.at[1])
    load_w('2_0', w2_hbm.at[0], wb, wb_sem.at[0])
    load_w('1_1', w1_hbm.at[1], wa.at[2], wa_sem.at[2])

    barrier = pltpu.get_barrier_semaphore()
    peers = row_peers + [p for p in col_peers if p[2]]
    for p in peers:
        pl.semaphore_signal(barrier, inc=1, device_id=dev(*p), device_id_type=MESH)
    pl.semaphore_wait(barrier, len(peers))
    tok_cp.wait()

    for dj in range(1, ny):
        send(meta_ref, ymeta.at[ny - dj], meta_send.at[0], ymeta_recv, (0, 0, dj))
    for dx in range(1, nx):
        send(meta_ref, xmeta.at[nx - dx], meta_send.at[1], xmeta_recv, (dx, 0, 0))

    def send_own(k):
        send(ag.at[0, :, cols(k)], ag.at[ny - 1, :, cols(k)], own_send, dn_recv.at[k], (0, 0, 1))
        send(ag.at[0, :, cols(k)], ag.at[1, :, cols(k)], own_send, up_recv.at[k], (0, 0, ny - 1))

    def forward(k):
        half = t_cnt // 2
        wait_bytes(ag.at[ny - 1, :, cols(k)], dn_recv.at[k])
        src = ag.at[ny - 1, pl.ds(0, half), cols(k)]
        send(src, ag.at[2, pl.ds(0, half), cols(k)], fwd_send, far_recv.at[k], (0, 0, 1))
        wait_bytes(ag.at[1, :, cols(k)], up_recv.at[k])
        src = ag.at[1, pl.ds(half, half), cols(k)]
        send(src, ag.at[2, pl.ds(half, half), cols(k)], fwd_send, far_recv.at[k], (0, 0, ny - 1))

    send_own(0)
    send_own(1)

    upper = (lax.broadcasted_iota(jnp.int32, (t_cnt, t_cnt), 0)
             < lax.broadcasted_iota(jnp.int32, (t_cnt, t_cnt), 1)).astype(F32).astype(BF)

    def vec_of(scalars):
        r_io = lax.broadcasted_iota(jnp.int32, (len(scalars), t_cnt), 0)
        v = jnp.zeros((len(scalars), t_cnt), jnp.int32)
        for r, s in enumerate(scalars):
            v = jnp.where(r_io == r, s, v)
        return v.astype(F32)

    def chosen(meta, evec):
        hit = jnp.zeros(evec.shape, F32)
        for q in range(top_k):
            hit = jnp.where(meta[q:q + 1, :] == evec, 1.0, hit)
        return hit

    def one_hot(key, n):
        m = key.shape[0]
        io = lax.broadcasted_iota(jnp.int32, (m, n, t_cnt), 1).astype(F32)
        return key[:, None, :] == io

    e_disp = []
    for l in range(e_loc):
        for dx in range(nx):
            for dc in range(NC):
                gg, jj = at(dx, dc, 0)
                e_disp.append(gg * e_grp + jj * e_loc + l)
    e_disp = vec_of(e_disp)

    g_lo = vec_of([at(dx, dc, 0)[0] * e_grp for dx in range(nx) for dc in range(NC)])
    own = meta_ref[...]
    hit = jnp.zeros(g_lo.shape, F32)
    for q in range(top_k):
        row = own[q:q + 1, :]
        hit = jnp.where((row >= g_lo) & (row < g_lo + e_grp), 1.0, hit)
    key = jnp.where(hit > 0.0, dot(hit.astype(BF), upper), -1.0)
    ft = jnp.where(one_hot(key, cap_g), 1.0, 0.0).astype(BF).reshape(nd * cap_g, t_cnt)
    eye = (lax.broadcasted_iota(jnp.int32, (t_cnt, t_cnt), 0)
           == lax.broadcasted_iota(jnp.int32, (t_cnt, t_cnt), 1)).astype(F32).astype(BF)
    fmat[...] = dot_nt(eye, ft).astype(BF)

    ymeta[0] = own
    xmeta[0] = own
    wait_bytes(ymeta.at[pl.ds(1, ny - 1)], ymeta_recv)
    for s in range(ny):
        hit = chosen(ymeta[s], e_disp)
        key = jnp.where(hit > 0.0, dot(hit.astype(BF), upper) + s * cap_e, -1.0)
        for l in range(e_loc):
            oh = jnp.where(one_hot(key[l * nd:(l + 1) * nd], ny * cap_e), 1.0, 0.0)
            smat[l, :, s * t_cnt:(s + 1) * t_cnt] = oh.astype(BF).reshape(rows, t_cnt)

    def select(l, k):
        r = dot(smat[l], ag[:, :, cols(k)].reshape(ny * t_cnt, cw)).astype(BF)
        r = r.reshape(nd, ny * cap_e, cw)
        sel[l, :, :, cols(k)] = r
        xin[l, 0, :, cols(k)] = r[0]
        for dx, dc, _ in far_first:
            slot = ((nx - dx) % nx) * NC + dc
            send(sel.at[l, dx * NC + dc, :, cols(k)], xin.at[l, slot, :, cols(k)],
                 disp_send.at[l], disp_recv.at[l], (dx, dc, 0))

    for k in range(nk):
        forward(k)
        if k + 2 < nk:
            send_own(k + 2)
        if k >= 1:
            wait_bytes(ag.at[2, :, cols(k - 1)], far_recv.at[k - 1])
            select(0, k - 1)
    wait_bytes(ag.at[2, :, cols(nk - 1)], far_recv.at[nk - 1])
    select(0, nk - 1)
    for l in range(1, e_loc):
        for k in range(nk):
            select(l, k)

    wait_bytes(xmeta.at[pl.ds(1, nx - 1)], xmeta_recv)
    gates = 8
    for rg in range(NC):
        e_vec = []
        for dj in range(ny):
            for l in range(e_loc):
                gg, jj = at(0, rg, dj)
                e_vec.append(gg * e_grp + jj * e_loc + l)
        e_vec = vec_of(e_vec)
        gs_parts = []
        w_parts = [[], [], []]
        for s in range(nx):
            m = xmeta[s]
            hit = chosen(m, e_vec)
            gate = jnp.zeros(e_vec.shape, F32)
            for q in range(top_k):
                gate = jnp.where(m[q:q + 1, :] == e_vec, m[gates + q:gates + q + 1, :], gate)
            key = jnp.where(hit > 0.0, dot(hit.astype(BF), upper) + s * cap_e, -1.0)
            any_hit = jnp.max(hit, axis=0, keepdims=True)
            g_hit = jnp.broadcast_to(any_hit, hit.shape)
            g_rank = dot(g_hit.astype(BF), upper)[0:1, :]
            g_key = jnp.where(any_hit > 0.0, g_rank + s * cap_g, -1.0)
            g_io = lax.broadcasted_iota(jnp.int32, (nx * cap_g, t_cnt), 0).astype(F32)
            gs_parts.append(jnp.where(g_key == g_io, 1.0, 0.0).astype(BF))
            g1 = gate.astype(BF)
            rest = gate - g1.astype(F32)
            g2 = rest.astype(BF)
            g3 = (rest - g2.astype(F32)).astype(BF)
            oh = one_hot(key, nx * cap_e)
            for part, gp in zip(w_parts, (g1, g2, g3)):
                w = jnp.where(oh, gp.astype(F32)[:, None, :], 0.0)
                part.append(w.astype(BF).reshape(e_grp * nx * cap_e, t_cnt))
        gs = jnp.concatenate(gs_parts, axis=1)
        n_g = nx * cap_g
        for i in range(3):
            w = jnp.concatenate(w_parts[i], axis=1)
            cmat[rg, i * n_g:(i + 1) * n_g, :] = dot_nt(gs, w).astype(BF)

    nw = 256
    slots = {0: (0, 1), 1: (2, 0)}
    for l in range(e_loc):
        s1, s3 = slots[l]
        wait_bytes(xin.at[l, pl.ds(1, nd - 1)], disp_recv.at[l])
        wcopies['1_%d' % l].wait()
        wcopies['3_%d' % l].wait()

        def h_body(n, carry):
            cs = pl.ds(pl.multiple_of(n * nw, nw), nw)
            xr = xin[l].reshape(rows, d_model)
            h1 = dot(xr, wa[s1, :, cs])
            h3 = dot(xr, wa[s3, :, cs])
            act[:, cs] = (jax.nn.silu(h1) * h3).astype(BF)
            return carry

        lax.fori_loop(0, ff // nw, h_body, 0)
        if l == 0:
            load_w('3_1', w3_hbm.at[1], wa.at[0], wa_sem.at[0])

        def p_body(n, carry):
            cs = pl.ds(pl.multiple_of(n * cw, cw), cw)
            actp[:, cs] = dot(perm_ref[...], act[:, cs]).astype(BF)
            return carry

        lax.fori_loop(0, ff // cw, p_body, 0)
        wcopies['2_%d' % l].wait()
        for k in range(nk):
            o = dot(actp[...], wb[:, cols(k)]).astype(BF).reshape(NC * ny, nx * cap_e, cw)
            out[l, :, :, cols(k)] = o
            eb[0, l, :, cols(k)] = o[0]
            for _, dc, dj in col_far_first:
                slot = dc * ny + (ny - dj) % ny
                send(out.at[l, dc * ny + dj, :, cols(k)], eb.at[slot, l, :, cols(k)],
                     comb_send.at[l], comb_recv.at[l, k], (0, dc, dj))
        if l == 0:
            load_w('2_1', w2_hbm.at[1], wb, wb_sem.at[0])

    def merge(k):
        n_g = nx * cap_g
        for l in range(e_loc):
            wait_bytes(eb.at[pl.ds(1, NC * ny - 1), l, :, cols(k)], comb_recv.at[l, k])
        for rg in range(NC):
            e = eb[rg * ny:(rg + 1) * ny, :, :, cols(k)].reshape(ny * e_loc * nx * cap_e, cw)
            r = dot(cmat[rg], e)
            r = (r[0:n_g] + r[n_g:2 * n_g] + r[2 * n_g:3 * n_g]).astype(BF).reshape(nx, cap_g, cw)
            gsum[:, rg, :, cols(k)] = r
            grec[0, rg, :, cols(k)] = r[0]
        for dx in sorted(range(1, nx), key=lambda d: -min(d, nx - d)):
            send(gsum.at[dx, :, :, cols(k)], grec.at[nx - dx, :, :, cols(k)],
                 fin_send, fin_recv.at[k], (dx, 0, 0))

    def final(k):
        wait_bytes(grec.at[pl.ds(1, nx - 1), :, :, cols(k)], fin_recv.at[k])
        g = grec[:, :, :, cols(k)].reshape(nd * cap_g, cw)
        y_ref[:, cols(k)] = dot(fmat[...], g).astype(BF)

    for k in range(nk):
        merge(k)
        if k >= 1:
            final(k - 1)
    final(nk - 1)

    wait_bytes(ymeta.at[pl.ds(1, ny - 1)], meta_send.at[0])
    wait_bytes(xmeta.at[pl.ds(1, nx - 1)], meta_send.at[1])
    wait_bytes(ag.at[pl.ds(0, 2)], own_send)
    wait_bytes(ag.at[0], fwd_send)
    for l in range(e_loc):
        wait_bytes(sel.at[l, pl.ds(1, nd - 1)], disp_send.at[l])
        wait_bytes(out.at[l, pl.ds(1, NC * ny - 1)], comb_send.at[l])
    wait_bytes(gsum.at[pl.ds(1, nx - 1)], fin_send)


def solution(mesh):
    n_grp = mesh.shape['grp']
    ny = mesh.shape['ing']
    nx = n_grp // NC
    row_spec = P(('dp', 'grp', 'ing'))
    exp_spec = P(('grp', 'ing'))

    def local_fn(tokens, expert_ids, gate_vals, w_one, w_three, w_two):
        t_cnt, d_model = tokens.shape
        m_groups, per_group = expert_ids.shape[1:]
        top_k = m_groups * per_group
        e_loc, _, ff = w_one.shape
        e_grp = e_loc * ny
        cap_g = (t_cnt * m_groups + n_grp - 1) // n_grp
        cap_e = (cap_g * per_group + e_grp - 1) // e_grp
        cw = 512
        nk = d_model // cw
        rows = n_grp * ny * cap_e
        dims = (t_cnt, d_model, ff, nx, ny, e_loc, e_grp, cap_g, cap_e, top_k, cw)

        ids_t = expert_ids.reshape(t_cnt, top_k).astype(F32).T
        gate_t = gate_vals.reshape(t_cnt, top_k).T
        pad = ((0, 8 - top_k), (0, 0))
        meta = jnp.concatenate([jnp.pad(ids_t, pad, constant_values=-1.0), jnp.pad(gate_t, pad)], axis=0)

        o = lax.broadcasted_iota(jnp.int32, (rows, rows), 0)
        i = lax.broadcasted_iota(jnp.int32, (rows, rows), 1)
        blk_o, q = o // cap_e, o % cap_e
        rx, rest = blk_o % nx, blk_o // nx
        rj, rc = rest % ny, rest // ny
        perm = (i == ((rx * NC + rc) * ny + rj) * cap_e + q).astype(BF)

        vm, dma = pltpu.VMEM, pltpu.SemaphoreType.DMA
        hbm = pl.BlockSpec(memory_space=pltpu.HBM)
        vmem = pl.BlockSpec(memory_space=pltpu.VMEM)
        blk = nx * cap_e
        return pl.pallas_call(
            functools.partial(moe_kernel, dims),
            out_shape=jax.ShapeDtypeStruct((t_cnt, d_model), BF),
            in_specs=[hbm, vmem, vmem, hbm, hbm, hbm],
            out_specs=vmem,
            scratch_shapes=[
                vm((3, d_model, ff), BF), vm((ff, d_model), BF),
                vm((ny, t_cnt, d_model), BF), vm((ny, 16, t_cnt), F32), vm((nx, 16, t_cnt), F32),
                vm((e_loc, n_grp, ny * cap_e, d_model), BF), vm((e_loc, n_grp, ny * cap_e, d_model), BF),
                vm((rows, ff), BF), vm((rows, ff), BF),
                vm((e_loc, NC * ny, blk, d_model), BF), vm((NC * ny, e_loc, blk, d_model), BF),
                vm((nx, NC, cap_g, d_model), BF), vm((nx, NC, cap_g, d_model), BF),
                vm((e_loc, rows, ny * t_cnt), BF), vm((NC, 3 * nx * cap_g, e_grp * blk), BF),
                vm((t_cnt, n_grp * cap_g), BF),
                dma((3,)), dma((1,)), dma, dma((2,)), dma, dma,
                dma, dma, dma((nk,)), dma((nk,)), dma((nk,)),
                dma((e_loc,)), dma((e_loc,)), dma((e_loc,)), dma((e_loc, nk)), dma, dma((nk,)),
            ],
            compiler_params=pltpu.CompilerParams(
                collective_id=0, has_side_effects=True, vmem_limit_bytes=67043328),
        )(tokens, meta, perm, w_one, w_three, w_two)

    return jax.shard_map(local_fn, mesh=mesh, in_specs=(row_spec, row_spec, row_spec, exp_spec, exp_spec, exp_spec), out_specs=row_spec, check_vma=False)
```

time: 226 us -> 112 us (0.50)
  blocking collectives: 127 us -> 0 us
  Pallas kernels: 0 us -> 106 us
  matrix products: 42.6 us -> 0 us
  waiting for transfers between devices: 21.8 us -> 0 us
  local copies, waits for them, and re-layouts: 18.6 us -> 2.67 us
  starting transfers between devices: 10.2 us -> 0 us
  other arithmetic: 5.46 us -> 2.67 us
    all_to_all x3 -> x0, blocking collectives: 127 us -> none  [the longest x1 49.8 us: local_fn(): x_exp = lax.all_to_all(x_fan, 'ing', 1, 1, tiled=True)]
    pallas_call x0 -> x1, Pallas kernels: none -> 106 us  [local_fn(): pl.pallas_call(functools.partial(moe_kernel, dims), out_shape=jax.ShapeDt...]
    dot_general x7 -> x0, matrix products: 42.6 us -> none  [the longest x1 21.3 us: local_fn(): jnp.einsum('lrf,lfd->lrd', act_bf, w_two, preferred_element_type=jnp.floa...]
    all_to_all x2 -> x0, waiting for transfers between devices: 21.8 us -> none  [the longest x1 19.3 us: local_fn(): x_recv = lax.all_to_all(x_send, 'grp', 0, 0, tiled=True)]
    all_to_all x2 -> x0, starting transfers between devices: 10.2 us -> none  [the longest x1 6.01 us: local_fn(): g_recv = lax.all_to_all(g_send, 'grp', 0, 0, tiled=True)]
    convert_element_type x4 -> x1, local copies, waits for them, and re-layouts: 8.62 us -> 0.01 us  [local_fn(): ids_t = expert_ids.reshape(t_cnt, top_k).astype(F32).T]
    all_to_all x2 -> x0, local copies, waits for them, and re-layouts: 4.55 us -> none  [the longest x1 4.04 us: local_fn(): x_exp = lax.all_to_all(x_fan, 'ing', 1, 1, tiled=True)]
    another operation x2 -> x0, other arithmetic: 3.94 us -> none  [the longest x1 3.77 us: local_fn(): exp_slot = jnp.cumsum(chosen_int, axis=1) - chosen_int]
  transfers between devices with their start and end apart: 2 -> 0, of which waited for: 2 -> 0; matrix products, arithmetic and copies ran while one was open for 3% -> 0% of each run, Pallas kernels for 0% -> 0%
where the time goes in v1:
time: 112 us; the launch traced here: 111 us
  Pallas kernels  106 us (95%)
  other arithmetic  2.67 us (2%)
  local copies, waits for them, and re-layouts  2.67 us (2%)
    pallas_call x1, Pallas kernels, local_fn(): pl.pallas_call(functools.partial(moe_kernel, dims), out_shape=jax.ShapeDt...  106 us

profile of v1, /device:TPU:97, one launch (start us, length us, event | category | flops | bytes accessed | tf_op | source)
XLA Modules:
  0.0 111.2 jit_solution(2734380207248377312)
XLA Ops:
  0.0 0.7 convert_element_type.11
  0.7 0.7 reshape.5
  1.4 0.6 select_maximum_fusion.meta_ref
  2.0 1.3 %fusion.15.perm_ref = bf16[384,384]{1,0:T(8,128)(2,1)} fusion(s32[384]{0:T(512)S(1)} %get-tuple-element.6, s32[384]{0:T(512)S(1)} %get-tuple-element.7, s32[384]{0:T(512)S(1)} %get-tuple-element.5, s32[384]{0:T(512)S(1)} %get-tuple-element.8, pred[384]{0:T(512)(128)(4,1)S(1)} %get-tuple-element.10, pred[384]{0:T(512)(128)(4,1)S(1)} %get-tuple-element.9), kind=kLoop, calls=%fused_computation.29 | loop fusion | flops 7077888 | bytes 301824 | tf_op jit(solution)/shard_map/convert_element_type | solution.py:322
  3.4 105.9 %shard_map.64 = bf16[128,2560]{1,0:T(8,128)(2,1)} custom-call(bf16[128,2560]{1,0:T(8,128)(2,1)} %tok_hbm.1, f32[16,128]{1,0:T(8,128)} %select_maximum_fusion.meta_ref, bf16[384,384]{1,0:T(8,128)(2,1)} %fusion.15.perm_ref, bf16[2,2560,1536]{2,1,0:T(8,128)(2,1)} %w1_hbm.1, bf16[2,2560,1536]{2,1,0:T(8,128)(2,1)} %w3_hbm.1, bf16[2,1536,2560]{2,1,0:T(8,128)(2,1)} %w2_hbm.1), custom_call_target="tpu_custom_call" | custom-call | tf_op jit(solution)/shard_map/pallas_call | solution.py:328
  109.3 2.0 %copy.8 = bf16[128,2560]{1,0:T(8,128)(2,1)} copy(bf16[128,2560]{1,0:T(8,128)(2,1)} %shard_map.64) | data formatting | bytes 1310720
  (4 shorter events, 0.0 us)
